TPU v7x, 32 devices: a whole 2x2x4 slice. The times are simulated.
32 devices in a mesh: ctx: 4 (over y, x), head: 8 (over z, core).
Axes of the slice: x: 2, y: 2, z: 4, core: 2. Of those that a mesh axis runs over, the one named last changes fastest.
Arguments:
- queries: bfloat16 [512, 3072], P('ctx', 'head'), may hold values from -10 to 10
- latent: bfloat16 [512, 576], P('ctx'), may hold values from -10 to 10
- block_of: int32 [8], replicated, may hold values from 0 to 7, each once
- key_up: bfloat16 [16, 128, 512], P('head'), may hold values from -0.5 to 0.5
- value_up: bfloat16 [16, 512, 128], P('head'), may hold values from -0.25 to 0.25
- out_grad: bfloat16 [512, 2048], P('ctx', 'head'), may hold values from -6 to 6
Outputs:
- attended: bfloat16 [512, 2048], P('ctx', 'head')
- query_grad: bfloat16 [512, 3072], P('ctx', 'head')
- latent_grad: float32 [512, 576], P('ctx')
Inputs may be any that keep to these rules, and one draw needn't show every extreme that they name: `block_of`: a permutation of the 8 blocks.
All inputs are finite; a program needn't handle non-finite values.
Results may differ from a plain program's by a relative error of at most 0.0099.
Values may be sent and summed in bfloat16 or wider, within the bound.
No kernel may reach another device: no remote copies, remote signals or barrier semaphores. Data moves between devices by JAX's collectives and lax.ppermute only.
A program may use at most 64 MiB of HBM per device.

v0:
```python
import math
import jax
import jax.numpy as jnp
from jax import lax
from jax.sharding import PartitionSpec as P

BLK_DEV = 2


def on_device(queries, latent, block_of, key_up, value_up, out_grad):
    local_rows = queries.shape[0]
    head_count = key_up.shape[0]
    nope_width = key_up.shape[1]
    latent_width = key_up.shape[2]
    joined_width = latent.shape[1]
    rope_width = joined_width - latent_width
    value_width = value_up.shape[2]
    score_scale = 1.0 / math.sqrt(nope_width + rope_width)
    all_latent = lax.all_gather(latent, "ctx", axis=0, tiled=True)
    total_rows = all_latent.shape[0]
    block_rows = local_rows // BLK_DEV
    row_index = jnp.arange(total_rows, dtype=jnp.int32)
    owner = (row_index // block_rows)[:, None] == jnp.arange(block_of.shape[0], dtype=jnp.int32)[
        None, :
    ]
    all_positions = (
        jnp.sum(jnp.where(owner, block_of[None, :], 0), axis=1) * block_rows
        + row_index % block_rows
    )
    my_positions = lax.dynamic_slice_in_dim(
        all_positions, lax.axis_index("ctx") * local_rows, local_rows
    )
    visible = all_positions[None, :] <= my_positions[:, None]
    query_heads = jnp.transpose(
        queries.reshape(local_rows, head_count, nope_width + rope_width), (1, 0, 2)
    )
    q_latent = jnp.einsum(
        "htn,hnl->htl", query_heads[:, :, :nope_width], key_up, preferred_element_type=jnp.float32
    ).astype(jnp.bfloat16)
    q_joined = jnp.concatenate([q_latent, query_heads[:, :, nope_width:]], axis=2)
    scores = (
        jnp.einsum("htw,kw->htk", q_joined, all_latent, preferred_element_type=jnp.float32)
        * score_scale
    )
    scores = jnp.where(visible[None], scores, -1e30)
    row_max = jnp.max(scores, axis=2, keepdims=True)
    expo = jnp.exp(scores - row_max)
    probs = expo / jnp.sum(expo, axis=2, keepdims=True)
    probs_low = probs.astype(jnp.bfloat16)
    latent_part = all_latent[:, :latent_width]
    out_latent = jnp.einsum(
        "htk,kl->htl", probs_low, latent_part, preferred_element_type=jnp.float32
    ).astype(jnp.bfloat16)
    attended = jnp.einsum(
        "htl,hlv->htv", out_latent, value_up, preferred_element_type=jnp.float32
    ).astype(jnp.bfloat16)
    attended = jnp.transpose(attended, (1, 0, 2)).reshape(local_rows, head_count * value_width)
    grad_heads = jnp.transpose(out_grad.reshape(local_rows, head_count, value_width), (1, 0, 2))
    grad_latent = jnp.einsum(
        "htv,hlv->htl", grad_heads, value_up, preferred_element_type=jnp.float32
    ).astype(jnp.bfloat16)
    grad_probs = jnp.einsum(
        "htl,kl->htk", grad_latent, latent_part, preferred_element_type=jnp.float32
    )
    delta = jnp.sum(probs * grad_probs, axis=2, keepdims=True)
    grad_scores = (probs * (grad_probs - delta) * score_scale).astype(jnp.bfloat16)
    grad_joined = jnp.einsum(
        "htk,kw->htw", grad_scores, all_latent, preferred_element_type=jnp.float32
    )
    grad_nope = jnp.einsum(
        "htl,hnl->htn",
        grad_joined[:, :, :latent_width].astype(jnp.bfloat16),
        key_up,
        preferred_element_type=jnp.float32,
    ).astype(jnp.bfloat16)
    grad_query = jnp.concatenate(
        [grad_nope, grad_joined[:, :, latent_width:].astype(jnp.bfloat16)], axis=2
    )
    query_grad = jnp.transpose(grad_query, (1, 0, 2)).reshape(
        local_rows, head_count * (nope_width + rope_width)
    )
    key_terms = jnp.einsum("htk,htw->kw", grad_scores, q_joined, preferred_element_type=jnp.float32)
    value_terms = jnp.einsum(
        "htk,htl->kl", probs_low, grad_latent, preferred_element_type=jnp.float32
    )
    key_terms = key_terms + jnp.pad(value_terms, ((0, 0), (0, rope_width)))
    columns = lax.psum_scatter(key_terms, "head", scatter_dimension=1, tiled=True)
    owned = lax.psum_scatter(columns, "ctx", scatter_dimension=0, tiled=True)
    latent_grad = lax.all_gather(owned, "head", axis=1, tiled=True)
    return (attended, query_grad, latent_grad)


def solution(mesh):
    return jax.shard_map(
        on_device,
        mesh=mesh,
        in_specs=(
            P("ctx", "head"),
            P("ctx", None),
            P(),
            P("head", None, None),
            P("head", None, None),
            P("ctx", "head"),
        ),
        out_specs=(P("ctx", "head"), P("ctx", "head"), P("ctx", None)),
        check_vma=False,
    )
```

profile of v0, /device:TPU:0, one launch (start us, length us, event | category | flops | bytes accessed | tf_op | source)
XLA Modules:
  0.0 109.3 jit_solution(8177717170956661955)
XLA Ops:
  7.2 0.0 copy-start
  7.2 0.0 copy-start.2
  7.2 0.0 copy-start.3
  7.2 0.0 reduce-scatter.3.cloned.1.call-start
  7.3 0.8 select_reduce_fusion
  8.1 0.1 dynamic_slice.3
  8.1 0.1 broadcast_compare_fusion
  8.3 1.0 copy.29
  9.3 0.1 copy.30
  9.4 1.2 %convolution_convert_fusion.3 = bf16[2,128,512]{2,1,0:T(8,128)(2,1)S(1)} fusion(bf16[2,128,512]{2,1,0:T(8,128)(2,1)} %param.9, bf16[2,128,192]{2,1,0:T(8,128)(2,1)S(1)} %bitcast.45), kind=kOutput, calls=%fused_computation.16 | convolution fusion | flops 33685504 | bytes 589824 | tf_op jit(solution)/shard_map/htn,hnl->htl/dot_general | solution.py:37
  10.6 0.0 copy-done.2
  10.6 11.8 %all_gather.6 = bf16[512,576]{0,1:T(8,128)(2,1)S(1)} all-gather(bf16[128,576]{0,1:T(8,128)(2,1)S(1)} %copy-done.2), channel_id=1, replica_groups=mesh['ctx'=4,'head'=8] {'ctx'}, dimensions={0}, use_global_device_ids=true | all-gather | bytes 737280 | tf_op jit(solution)/shard_map/all_gather | solution.py:19
  22.4 0.0 copy-done
  22.4 0.0 copy-done.3
  22.4 0.2 convolution_convert_fusion.1
  22.6 0.3 fusion.18
  22.9 0.4 fusion.5
  23.3 0.4 fusion.41
  23.8 1.7 %convolution_bitcast_fusion.1 = f32[512,512]{0,1:T(8,128)} fusion(bf16[2,128,512]{2,1,0:T(8,128)(2,1)S(1)} %convolution_convert_fusion.1, f32[2,128]{1,0:T(2,128)S(1)} %get-tuple-element.12, f32[2,128,512]{2,1,0:T(8,128)S(1)} %fusion.5), kind=kOutput, calls=%fused_computation.3 | convolution fusion | flops 134611712 | bytes 1836032 | tf_op jit(solution)/shard_map/htk,htl->kl/dot_general | solution.py:83
  25.5 3.6 %fusion.2 = f32[512,576]{0,1:T(8,128)} fusion(f32[512,512]{0,1:T(8,128)} %convolution_bitcast_fusion.1, f32[2,128,512]{2,1,0:T(8,128)S(1)} %fusion.18, bf16[2,128,64]{2,1,0:T(8,128)(2,1)S(1)} %slice.23, bf16[2,128,512]{2,1,0:T(8,128)(2,1)S(1)} %convolution_convert_fusion.3, f32[2,128,512]{2,1,0:T(8,128)S(1)} %get-tuple-element.13, ...), kind=kOutput, calls=%fused_computation.4 | convolution fusion | flops 152797952 | bytes 3572736 | tf_op jit(solution)/shard_map/htk,htw->kw/dot_general | solution.py:82
  29.1 0.0 reduce-scatter.3.cloned.1.call-update
  29.1 0.0 reduce-scatter.5.cloned.1.call-start
  29.2 0.9 fusion.11
  30.1 0.7 copy.39
  30.8 0.0 copy-start.1
  30.8 0.9 convolution_convert_fusion
  31.7 30.9 %reduce-scatter.3.cloned.1.call-done = f32[512,72]{0,1:T(8,128)} async-done(((f32[512,576]{0,1:T(8,128)}), f32[512,72]{0,1:T(8,128)}) %reduce-scatter.3.cloned.1.call-update) | async-done | bytes 147472 | tf_op jit(solution)/shard_map/reduce_scatter | solution.py:87
  62.6 0.0 reduce-scatter.5.cloned.1.call-update
  62.6 0.0 copy-done.1
  62.6 0.2 convolution_convert_fusion.4
  62.8 0.8 copy.40
  63.6 23.6 %reduce-scatter.5.cloned.1.call-done = f32[128,72]{0,1:T(8,128)} async-done(((f32[512,72]{0,1:T(8,128)}), f32[128,72]{0,1:T(8,128)}) %reduce-scatter.5.cloned.1.call-update) | async-done | bytes 36880 | tf_op jit(solution)/shard_map/reduce_scatter | solution.py:88
  87.2 14.6 %all_gather.7 = f32[128,576]{0,1:T(8,128)S(1)} all-gather(f32[128,72]{0,1:T(8,128)} %reduce-scatter.5.cloned.1.call-done), channel_id=1, replica_groups=mesh['ctx'=4,'head'=8] {'head'}, dimensions={1}, use_global_device_ids=true | all-gather | bytes 331776 | tf_op jit(solution)/shard_map/all_gather | solution.py:89
  101.7 0.7 copy.56
  (5 shorter events, 0.0 us)
Async XLA Ops:
  7.2 15.2 %copy-start = (bf16[2,512,128]{2,1,0:T(8,128)(2,1)S(1)}, bf16[2,512,128]{2,1,0:T(8,128)(2,1)}, u32[]{:S(2)}) copy-start(bf16[2,512,128]{2,1,0:T(8,128)(2,1)} %param.10) | copy-start | bytes 786436
  7.2 3.4 %copy-start.2 = (bf16[128,576]{0,1:T(8,128)(2,1)S(1)}, bf16[128,576]{0,1:T(8,128)(2,1)}, u32[]{:S(2)}) copy-start(bf16[128,576]{0,1:T(8,128)(2,1)} %param.7) | copy-start | bytes 442372
  7.2 15.2 %copy-start.3 = (bf16[128,256]{1,0:T(8,128)(2,1)S(1)}, bf16[128,256]{1,0:T(8,128)(2,1)}, u32[]{:S(2)}) copy-start(bf16[128,256]{1,0:T(8,128)(2,1)} %param.11) | copy-start | bytes 196612
  7.2 55.4 %reduce-scatter.3.cloned.1.call-start = ((), (), s32[]{:S(2)}) async-start(), calls=%async_computation.2 | async-start | bytes 1327104 | tf_op jit(solution)/shard_map/reduce_scatter | solution.py:87
  29.1 58.0 %reduce-scatter.5.cloned.1.call-start = ((), (), s32[]{:S(2)}) async-start(), calls=%async_computation.3 | async-start | bytes 184320 | tf_op jit(solution)/shard_map/reduce_scatter | solution.py:88
  30.8 31.8 %copy-start.1 = (bf16[2,128,512]{2,1,0:T(8,128)(2,1)S(1)}, bf16[2,128,512]{2,1,0:T(8,128)(2,1)}, u32[]{:S(2)}) copy-start(bf16[2,128,512]{2,1,0:T(8,128)(2,1)} %param.9) | copy-start | bytes 786436
Sparse Core Ops, SparseCore 0:
  29.3 33.2 reduce-scatter.2
  65.3 21.8 reduce-scatter.4
where the time goes:
time: 110 us; the launch traced here: 109 us
  waiting for transfers between devices  54.5 us (50%)
  blocking collectives  26.4 us (24%)
  between operations  14.2 us (13%)
  matrix products  9.4 us (9%)
  local copies, waits for them, and re-layouts  3.44 us (3%)
  other arithmetic  1.35 us (1%)
    reduce_scatter x1, waiting for transfers between devices, on_device(): lax.psum_scatter(key_terms, 'head', scatter_dimension=1, tiled=True)  30.9 us
    reduce_scatter x1, waiting for transfers between devices, on_device(): owned = lax.psum_scatter(columns, 'ctx', scatter_dimension=0, tiled=True)  23.6 us
    all_gather x1, blocking collectives, on_device(): latent_grad = lax.all_gather(owned, 'head', axis=1, tiled=True)  14.6 us
    all_gather x1, blocking collectives, on_device(): all_latent = lax.all_gather(latent, 'ctx', axis=0, tiled=True)  11.8 us
    dot_general x1, matrix products, on_device(): jnp.einsum('htk,htw->kw', grad_scores, q_joined, preferred_element_type=j...  3.62 us
    unnamed x12, local copies, waits for them, and re-layouts  3.24 us
  transfers between devices with their start and end apart: 2, of which 2 were waited for; matrix products, arithmetic and copies ran while one was open for 3% of the time, Pallas kernels for 0%

commit v1 on v0

--- a/solution.py
+++ b/solution.py
@@ -5,6 +5,12 @@
 from jax.sharding import PartitionSpec as P
 
 BLK_DEV = 2
+
+
+def assign_signs(local, out_dim):
+    state_now = list(local.shape[1:])
+    state_now[out_dim] *= local.shape[0]
+    return jnp.moveaxis(local, 0, out_dim).reshape(state_now)
 
 
 def on_device(queries, latent, block_of, key_up, value_up, out_grad):
@@ -86,7 +92,22 @@
     key_terms = key_terms + jnp.pad(value_terms, ((0, 0), (0, rope_width)))
     columns = lax.psum_scatter(key_terms, "head", scatter_dimension=1, tiled=True)
     owned = lax.psum_scatter(columns, "ctx", scatter_dimension=0, tiled=True)
-    latent_grad = lax.all_gather(owned, "head", axis=1, tiled=True)
+    cores_n = lax.axis_size("head")
+    rows = [(m, (m + 1) % cores_n) for m in range(cores_n)]
+    series = [(j0, u) for u, j0 in rows]
+    z2, tall = ([], [])
+    for idx in [*range(cores_n - 1)]:
+        if idx % 2 == 0:
+            now = lax.ppermute(z2[-1] if z2 else owned, axis_name="head", perm=rows)
+            z2.append(now)
+        else:
+            side_arr = lax.ppermute(tall[-1] if tall else owned, axis_name="head", perm=series)
+            tall.append(side_arr)
+    placed = jnp.stack([*z2[::-1], owned, *tall])
+    wide_out = lax.axis_index("head")
+    answer = wide_out - len(z2)
+    placed = placed[(jnp.arange(cores_n) - answer) % cores_n]
+    latent_grad = assign_signs(placed, 1)
     return (attended, query_grad, latent_grad)
 
 

time: 110 us -> 118 us (1.073)
  blocking collectives: 26.4 us -> 12.4 us
  waiting for transfers between devices: 54.5 us -> 66.3 us
  starting transfers between devices: 0.08 us -> 10.6 us
    all_gather x1 -> x0, blocking collectives: 14.6 us -> none  [on_device(): latent_grad = lax.all_gather(owned, 'head', axis=1, tiled=True)]
    ppermute x0 -> x7, starting transfers between devices: none -> 10.6 us  [the longest x3 10.6 us: on_device(): lax.ppermute(tall[-1] if tall else owned, axis_name='head', perm=series)]
    ppermute x0 -> x7, waiting for transfers between devices: none -> 10.1 us  [the longest x4 8.38 us: on_device(): now = lax.ppermute(z2[-1] if z2 else owned, axis_name='head', perm=rows)]
    reduce_scatter x1, waiting for transfers between devices: 30.9 us -> 33.3 us  [on_device(): lax.psum_scatter(key_terms, 'head', scatter_dimension=1, tiled=True)]
    gather x0 -> x1, local copies, waits for them, and re-layouts: none -> 1.28 us  [on_device(): placed = placed[(jnp.arange(cores_n) - answer) % cores_n]]
    unnamed x12 -> x18, local copies, waits for them, and re-layouts: 3.24 us -> 2.56 us
  transfers between devices with their start and end apart: 2 -> 9, of which waited for: 2 -> 8; matrix products, arithmetic and copies ran while one was open for 3% -> 3% of each run, Pallas kernels for 0% -> 0%
where the time goes in v1:
time: 118 us; the launch traced here: 117 us
  waiting for transfers between devices  66.3 us (56%)
  between operations  14.3 us (12%)
  blocking collectives  12.4 us (11%)
  starting transfers between devices  10.6 us (9%)
  matrix products  8.45 us (7%)
  local copies, waits for them, and re-layouts  4.04 us (3%)
  other arithmetic  1.31 us (1%)
    reduce_scatter x1, waiting for transfers between devices, on_device(): lax.psum_scatter(key_terms, 'head', scatter_dimension=1, tiled=True)  33.3 us
    reduce_scatter x1, waiting for transfers between devices, on_device(): owned = lax.psum_scatter(columns, 'ctx', scatter_dimension=0, tiled=True)  23 us
    all_gather x1, blocking collectives, on_device(): all_latent = lax.all_gather(latent, 'ctx', axis=0, tiled=True)  12.4 us
    ppermute x3, starting transfers between devices, on_device(): lax.ppermute(tall[-1] if tall else owned, axis_name='head', perm=series)  10.6 us
    ppermute x4, waiting for transfers between devices, on_device(): now = lax.ppermute(z2[-1] if z2 else owned, axis_name='head', perm=rows)  8.38 us
    dot_general x1, matrix products, on_device(): jnp.einsum('htk,htw->kw', grad_scores, q_joined, preferred_element_type=j...  3.62 us
    unnamed x18, local copies, waits for them, and re-layouts  2.56 us
  transfers between devices with their start and end apart: 9, of which 8 were waited for; matrix products, arithmetic and copies ran while one was open for 3% of the time, Pallas kernels for 0%

profile of v1, /device:TPU:0, one launch (start us, length us, event | category | flops | bytes accessed | tf_op | source)
XLA Modules:
  0.0 117.5 jit_solution(4114440800176025798)
XLA Ops:
  7.2 0.0 copy-start
  7.2 0.0 copy-start.1
  7.2 0.0 reduce-scatter.3.cloned.1.call-start
  7.2 12.4 %all_gather.3 = bf16[512,576]{0,1:T(8,128)(2,1)S(1)} all-gather(bf16[128,576]{0,1:T(8,128)(2,1)} %param.7), channel_id=1, replica_groups=mesh['ctx'=4,'head'=8] {'ctx'}, dimensions={0}, use_global_device_ids=true | all-gather | bytes 737280 | tf_op jit(solution)/shard_map/all_gather | solution.py:25
  19.7 0.7 select_reduce_fusion
  20.4 0.1 dynamic_slice.3
  20.5 0.1 broadcast_compare_fusion
  20.6 1.0 copy.29
  21.6 0.1 copy.30
  21.8 0.0 copy-done.1
  21.8 0.2 convolution_convert_fusion.3
  22.0 0.0 copy-start.2
  22.0 0.4 fusion.5
  22.4 0.4 fusion.43
  22.8 0.0 copy-done
  22.8 0.0 copy-done.2
  22.8 0.2 convolution_convert_fusion.1
  23.1 0.3 fusion.18
  23.4 1.7 %convolution_bitcast_fusion.1 = f32[512,512]{0,1:T(8,128)} fusion(bf16[2,128,512]{2,1,0:T(8,128)(2,1)S(1)} %convolution_convert_fusion.1, f32[2,128]{1,0:T(2,128)S(1)} %get-tuple-element.12, f32[2,128,512]{2,1,0:T(8,128)S(1)} %fusion.5), kind=kOutput, calls=%fused_computation.4 | convolution fusion | flops 134611712 | bytes 1836032 | tf_op jit(solution)/shard_map/htk,htl->kl/dot_general | solution.py:89
  25.1 3.6 %fusion.2 = f32[512,576]{0,1:T(8,128)} fusion(f32[512,512]{0,1:T(8,128)} %convolution_bitcast_fusion.1, f32[2,128,512]{2,1,0:T(8,128)S(1)} %fusion.18, bf16[2,128,64]{2,1,0:T(8,128)(2,1)S(1)} %slice.25, bf16[2,128,512]{2,1,0:T(8,128)(2,1)S(1)} %convolution_convert_fusion.3, f32[2,128,512]{2,1,0:T(8,128)S(1)} %get-tuple-element.13, ...), kind=kOutput, calls=%fused_computation.5 | convolution fusion | flops 152797952 | bytes 3572736 | tf_op jit(solution)/shard_map/htk,htw->kw/dot_general | solution.py:88
  28.8 0.0 reduce-scatter.3.cloned.1.call-update
  28.8 0.0 reduce-scatter.5.cloned.1.call-start
  28.8 33.3 %reduce-scatter.3.cloned.1.call-done = f32[512,72]{0,1:T(8,128)} async-done(((f32[512,576]{0,1:T(8,128)}), f32[512,72]{0,1:T(8,128)}) %reduce-scatter.3.cloned.1.call-update) | async-done | bytes 147472 | tf_op jit(solution)/shard_map/reduce_scatter | solution.py:93
  62.1 0.0 reduce-scatter.5.cloned.1.call-update
  62.1 0.9 fusion.11
  63.0 0.9 convolution_convert_fusion
  63.9 23.0 %reduce-scatter.5.cloned.1.call-done = f32[128,72]{0,1:T(8,128)} async-done(((f32[512,72]{0,1:T(8,128)}), f32[128,72]{0,1:T(8,128)}) %reduce-scatter.5.cloned.1.call-update) | async-done | bytes 36880 | tf_op jit(solution)/shard_map/reduce_scatter | solution.py:94
  86.8 0.0 copy-start.3
  86.8 0.0 collective-permute-start
  86.8 0.2 convolution_convert_fusion.4
  87.1 5.2 %collective-permute-done = f32[128,72]{0,1:T(8,128)S(1)} collective-permute-done((f32[128,72]{0,1:T(8,128)}, f32[128,72]{0,1:T(8,128)S(1)}, u32[]{:S(2)}, u32[]{:S(2)}) %collective-permute-start) | collective-permute-done | bytes 36896 | tf_op jit(solution)/shard_map/ppermute | solution.py:101
  92.2 0.0 collective-permute-start.1
  92.3 3.6 %collective-permute-start.4 = (f32[128,72]{0,1:T(8,128)}, f32[128,72]{0,1:T(8,128)S(1)}, u32[]{:S(2)}, u32[]{:S(2)}) collective-permute-start(f32[128,72]{0,1:T(8,128)} %reduce-scatter.5.cloned.1.call-done), channel_id=1, source_target_pairs={{1,0},{2,1},{3,2},{4,3},{5,4},{6,5},{7,6},{0,7},{9,8},{10,9},{11,1... | collective-permute-start | bytes 110600 | tf_op jit(solution)/shard_map/ppermute | solution.py:104
  95.8 1.7 %collective-permute-done.1 = f32[128,72]{0,1:T(8,128)S(1)} collective-permute-done((f32[128,72]{0,1:T(8,128)S(1)}, f32[128,72]{0,1:T(8,128)S(1)}, u32[]{:S(2)}, u32[]{:S(2)}) %collective-permute-start.1) | collective-permute-done | bytes 36896 | tf_op jit(solution)/shard_map/ppermute | solution.py:101
  97.5 0.0 collective-permute-start.2
  97.5 0.3 collective-permute-done.4
  97.8 3.4 %collective-permute-start.5 = (f32[128,72]{0,1:T(8,128)S(1)}, f32[128,72]{0,1:T(8,128)S(1)}, u32[]{:S(2)}, u32[]{:S(2)}) collective-permute-start(f32[128,72]{0,1:T(8,128)S(1)} %collective-permute-done.4), channel_id=1, source_target_pairs={{1,0},{2,1},{3,2},{4,3},{5,4},{6,5},{7,6},{0,7},{9,8},{10,9},{11,1... | collective-permute-start | bytes 110600 | tf_op jit(solution)/shard_map/ppermute | solution.py:104
  101.2 1.4 %collective-permute-done.2 = f32[128,72]{0,1:T(8,128)S(1)} collective-permute-done((f32[128,72]{0,1:T(8,128)S(1)}, f32[128,72]{0,1:T(8,128)S(1)}, u32[]{:S(2)}, u32[]{:S(2)}) %collective-permute-start.2) | collective-permute-done | bytes 36896 | tf_op jit(solution)/shard_map/ppermute | solution.py:101
  102.7 0.0 collective-permute-start.3
  102.7 0.7 copy.39
  103.4 0.8 copy.40
  104.2 0.0 collective-permute-done.5
  104.2 3.5 %collective-permute-start.6 = (f32[128,72]{0,1:T(8,128)S(1)}, f32[128,72]{0,1:T(8,128)S(1)}, u32[]{:S(2)}, u32[]{:S(2)}) collective-permute-start(f32[128,72]{0,1:T(8,128)S(1)} %collective-permute-done.5), channel_id=1, source_target_pairs={{1,0},{2,1},{3,2},{4,3},{5,4},{6,5},{7,6},{0,7},{9,8},{10,9},{11,1... | collective-permute-start | bytes 110600 | tf_op jit(solution)/shard_map/ppermute | solution.py:104
  107.7 0.1 collective-permute-done.3
  107.9 0.0 copy-done.3
  107.9 1.4 %collective-permute-done.6 = f32[128,72]{0,1:T(8,128)S(1)} collective-permute-done((f32[128,72]{0,1:T(8,128)S(1)}, f32[128,72]{0,1:T(8,128)S(1)}, u32[]{:S(2)}, u32[]{:S(2)}) %collective-permute-start.6) | collective-permute-done | bytes 36896 | tf_op jit(solution)/shard_map/ppermute | solution.py:104
  109.4 1.3 %gather_fusion = f32[8,128,72]{1,2,0:T(8,128)} fusion(f32[8,128,72]{1,2,0:T(8,128)S(1)} %bitcast_dynamic-update-slice_fusion, s32[1024]{0:T(1024)S(1)} %pad_clamp_fusion), kind=kCustom, calls=%fused_computation | custom fusion | bytes 589856 | tf_op jit(solution)/shard_map/gather | solution.py:109
  (15 shorter events, 0.1 us)
Async XLA Ops:
  7.2 15.7 %copy-start = (bf16[2,512,128]{2,1,0:T(8,128)(2,1)S(1)}, bf16[2,512,128]{2,1,0:T(8,128)(2,1)}, u32[]{:S(2)}) copy-start(bf16[2,512,128]{2,1,0:T(8,128)(2,1)} %param.10) | copy-start | bytes 786436
  7.2 14.6 %copy-start.1 = (bf16[2,128,512]{2,1,0:T(8,128)(2,1)S(1)}, bf16[2,128,512]{2,1,0:T(8,128)(2,1)}, u32[]{:S(2)}) copy-start(bf16[2,128,512]{2,1,0:T(8,128)(2,1)} %param.9) | copy-start | bytes 786436
  7.2 54.9 %reduce-scatter.3.cloned.1.call-start = ((), (), s32[]{:S(2)}) async-start(), calls=%async_computation.2 | async-start | bytes 1327104 | tf_op jit(solution)/shard_map/reduce_scatter | solution.py:93
  22.0 0.8 copy-start.2
  28.8 58.1 %reduce-scatter.5.cloned.1.call-start = ((), (), s32[]{:S(2)}) async-start(), calls=%async_computation.3 | async-start | bytes 184320 | tf_op jit(solution)/shard_map/reduce_scatter | solution.py:94
  86.8 21.1 %copy-start.3 = (f32[128,72]{0,1:T(8,128)S(1)}, f32[128,72]{0,1:T(8,128)}, u32[]{:S(2)}) copy-start(f32[128,72]{0,1:T(8,128)} %reduce-scatter.5.cloned.1.call-done) | copy-start | bytes 110596
  86.8 5.4 %collective-permute-start = (f32[128,72]{0,1:T(8,128)}, f32[128,72]{0,1:T(8,128)S(1)}, u32[]{:S(2)}, u32[]{:S(2)}) collective-permute-start(f32[128,72]{0,1:T(8,128)} %reduce-scatter.5.cloned.1.call-done), channel_id=1, source_target_pairs={{0,1},{1,2},{2,3},{3,4},{4,5},{5,6},{6,7},{7,0},{8,9},{9,10},{10,1... | collective-permute-start | bytes 110600 | tf_op jit(solution)/shard_map/ppermute | solution.py:101
  92.2 5.3 %collective-permute-start.1 = (f32[128,72]{0,1:T(8,128)S(1)}, f32[128,72]{0,1:T(8,128)S(1)}, u32[]{:S(2)}, u32[]{:S(2)}) collective-permute-start(f32[128,72]{0,1:T(8,128)S(1)} %collective-permute-done), channel_id=1, source_target_pairs={{0,1},{1,2},{2,3},{3,4},{4,5},{5,6},{6,7},{7,0},{8,9},{9,10},{10,1... | collective-permute-start | bytes 110600 | tf_op jit(solution)/shard_map/ppermute | solution.py:101
  92.3 5.5 %collective-permute-start.4 = (f32[128,72]{0,1:T(8,128)}, f32[128,72]{0,1:T(8,128)S(1)}, u32[]{:S(2)}, u32[]{:S(2)}) collective-permute-start(f32[128,72]{0,1:T(8,128)} %reduce-scatter.5.cloned.1.call-done), channel_id=1, source_target_pairs={{1,0},{2,1},{3,2},{4,3},{5,4},{6,5},{7,6},{0,7},{9,8},{10,9},{11,1... | collective-permute-start | bytes 110600 | tf_op jit(solution)/shard_map/ppermute | solution.py:104
  97.5 5.2 %collective-permute-start.2 = (f32[128,72]{0,1:T(8,128)S(1)}, f32[128,72]{0,1:T(8,128)S(1)}, u32[]{:S(2)}, u32[]{:S(2)}) collective-permute-start(f32[128,72]{0,1:T(8,128)S(1)} %collective-permute-done.1), channel_id=1, source_target_pairs={{0,1},{1,2},{2,3},{3,4},{4,5},{5,6},{6,7},{7,0},{8,9},{9,10},{10,1... | collective-permute-start | bytes 110600 | tf_op jit(solution)/shard_map/ppermute | solution.py:101
  97.8 6.4 %collective-permute-start.5 = (f32[128,72]{0,1:T(8,128)S(1)}, f32[128,72]{0,1:T(8,128)S(1)}, u32[]{:S(2)}, u32[]{:S(2)}) collective-permute-start(f32[128,72]{0,1:T(8,128)S(1)} %collective-permute-done.4), channel_id=1, source_target_pairs={{1,0},{2,1},{3,2},{4,3},{5,4},{6,5},{7,6},{0,7},{9,8},{10,9},{11,1... | collective-permute-start | bytes 110600 | tf_op jit(solution)/shard_map/ppermute | solution.py:104
  102.7 5.2 %collective-permute-start.3 = (f32[128,72]{0,1:T(8,128)S(1)}, f32[128,72]{0,1:T(8,128)S(1)}, u32[]{:S(2)}, u32[]{:S(2)}) collective-permute-start(f32[128,72]{0,1:T(8,128)S(1)} %collective-permute-done.2), channel_id=1, source_target_pairs={{0,1},{1,2},{2,3},{3,4},{4,5},{5,6},{6,7},{7,0},{8,9},{9,10},{10,1... | collective-permute-start | bytes 110600 | tf_op jit(solution)/shard_map/ppermute | solution.py:101
  104.2 5.2 %collective-permute-start.6 = (f32[128,72]{0,1:T(8,128)S(1)}, f32[128,72]{0,1:T(8,128)S(1)}, u32[]{:S(2)}, u32[]{:S(2)}) collective-permute-start(f32[128,72]{0,1:T(8,128)S(1)} %collective-permute-done.5), channel_id=1, source_target_pairs={{1,0},{2,1},{3,2},{4,3},{5,4},{6,5},{7,6},{0,7},{9,8},{10,9},{11,1... | collective-permute-start | bytes 110600 | tf_op jit(solution)/shard_map/ppermute | solution.py:104
Sparse Core Ops, SparseCore 0:
  28.9 33.1 reduce-scatter.2
  64.8 21.9 reduce-scatter.4
